TPU v7x, 128 devices: a whole 4x4x4 slice. The times are simulated.
128 devices in a mesh: rep: 1, dp: 16 (over z, y), ad: 8 (over x, core).
Axes of the slice: x: 4, y: 4, z: 4, core: 2. Of those that a mesh axis runs over, the one named last changes fastest.
Arguments:
- x_rows: bfloat16 [65536, 3072], P(('rep', 'dp', 'ad'))
- adapter_id: int32 [65536], P(('rep', 'dp', 'ad'))
- w_gate: bfloat16 [3072, 8192], replicated
- w_up: bfloat16 [3072, 8192], replicated
- w_down: bfloat16 [8192, 3072], replicated
- a_gate: bfloat16 [16, 3072, 32], P('ad')
- b_gate: bfloat16 [16, 32, 8192], P('ad')
- a_up: bfloat16 [16, 3072, 32], P('ad')
- b_up: bfloat16 [16, 32, 8192], P('ad')
- a_down: bfloat16 [16, 8192, 32], P('ad')
- b_down: bfloat16 [16, 32, 3072], P('ad')
Outputs:
- output: bfloat16 [65536, 3072], P(('rep', 'dp', 'ad'))
All inputs are finite; a program needn't handle non-finite values.
Results may differ from a plain program's by a relative error of at most 0.00131.
Values are sent between devices in bfloat16 or wider.
A program may use at most 1 GiB of HBM per device.

v0:
```python
import jax
import jax.numpy as jnp
from jax import lax
from jax.sharding import PartitionSpec as P

value_a10 = 32
CAP_MULT = 4


def route_plan(adapter_id, n_rows, group, n_local, capacity):
    owner = adapter_id // n_local
    tok_order = jnp.argsort(owner, stable=True)
    owner_sorted = jnp.take(owner, tok_order)
    counts = jnp.bincount(owner, length=group)
    starts = jnp.cumsum(counts) - counts
    slot_sorted = owner_sorted * capacity + jnp.arange(n_rows) - jnp.take(starts, owner_sorted)
    token_slot = jnp.take(slot_sorted, jnp.argsort(tok_order))
    within = jnp.arange(capacity)
    pick_index = jnp.minimum(starts[:, None] + within[None, :], n_rows - 1).reshape(-1)
    send_rows = jnp.take(tok_order, pick_index)
    filled = (within[None, :] < counts[:, None]).reshape(-1)
    send_local = jnp.where(filled, jnp.take(adapter_id, send_rows) % n_local, 0)
    return token_slot, send_rows, send_local


def solution(mesh):
    group = mesh.shape["ad"]
    tok_axes = ("rep", "dp", "ad")
    row_spec = P(tok_axes, None)
    owned = P("ad", None, None)

    def local_step(x_rows, adapter_id, w_gate, w_up, w_down, a_gate, b_gate, a_up, b_up, a_down, b_down):
        n_rows = x_rows.shape[0]
        n_local, _, rank = a_gate.shape
        d_ff = w_gate.shape[1]
        scale = value_a10 / rank
        capacity = (n_rows // group) * min(CAP_MULT, max(1, group // 2))
        token_slot, send_rows, send_local = route_plan(adapter_id, n_rows, group, n_local, capacity)
        local_recv = lax.all_to_all(send_local, "ad", 0, 0, tiled=True)
        select = (local_recv[:, None] == jnp.arange(n_local)[None, :]).astype(jnp.bfloat16)

        def low_rank(rows_in, a_mat, b_mat):
            low_proj = jnp.einsum("mk,akr->mar", rows_in, a_mat, preferred_element_type=jnp.float32)
            low_proj = low_proj.astype(jnp.bfloat16) * select[:, :, None]
            wide_proj = jnp.einsum("mar,arn->mn", low_proj, b_mat, preferred_element_type=jnp.float32)
            return (scale * wide_proj).astype(jnp.bfloat16)

        x_recv = lax.all_to_all(jnp.take(x_rows, send_rows, axis=0), "ad", 0, 0, tiled=True)
        gu_delta = jnp.concatenate([low_rank(x_recv, a_gate, b_gate), low_rank(x_recv, a_up, b_up)], axis=1)
        gu_token = jnp.take(lax.all_to_all(gu_delta, "ad", 0, 0, tiled=True), token_slot, axis=0)
        gate_pre = jnp.dot(x_rows, w_gate, preferred_element_type=jnp.float32) + gu_token[:, :d_ff].astype(jnp.float32)
        up_proj = jnp.dot(x_rows, w_up, preferred_element_type=jnp.float32) + gu_token[:, d_ff:].astype(jnp.float32)
        hidden = (jax.nn.silu(gate_pre) * up_proj).astype(jnp.bfloat16)
        h_recv = lax.all_to_all(jnp.take(hidden, send_rows, axis=0), "ad", 0, 0, tiled=True)
        down_delta = lax.all_to_all(low_rank(h_recv, a_down, b_down), "ad", 0, 0, tiled=True)
        down_token = jnp.take(down_delta, token_slot, axis=0)
        down_proj = jnp.dot(hidden, w_down, preferred_element_type=jnp.float32) + down_token.astype(jnp.float32)
        return (x_rows.astype(jnp.float32) + down_proj).astype(jnp.bfloat16)

    return jax.shard_map(local_step, mesh=mesh,
                         in_specs=(row_spec, P(tok_axes), P(), P(), P(), owned, owned, owned, owned, owned, owned),
                         out_specs=row_spec, check_vma=False)
```

profile of v0, /device:TPU:1, one launch (start us, length us, event | category | flops | bytes accessed | tf_op | source)
XLA Modules:
  0.0 1807.6 jit_solution(654648036893112879)
XLA Ops:
  0.8 4.1 scatter_custom_fusion
  5.7 3.8 sort.34
  9.5 13.2 gather_fusion.6
  22.7 11.1 gather_fusion.7
  34.5 5.8 all-to-all-start.1
  40.3 25.3 %gather_fusion = bf16[2048,3072]{1,0:T(8,128)(2,1)} fusion(bf16[512,3072]{1,0:T(8,128)(2,1)} %param.15, s32[2048]{0:T(1024)S(1)} %broadcast_clamp_fusion), kind=kCustom, calls=%fused_computation.4 | custom fusion | bytes 25174016 | tf_op jit(solution)/shard_map/jit(_take)/gather | solution.py:48
  65.6 10.9 broadcast_select_fusion.2
  76.5 5.6 all-to-all-start
  82.2 138.4 %all-to-all-done = bf16[8,256,3072]{2,1,0:T(8,128)(2,1)} async-done(((bf16[8,256,3072]{2,1,0:T(8,128)(2,1)}), bf16[8,256,3072]{2,1,0:T(8,128)(2,1)}, u32[]{:S(2)}, u32[]{:S(2)}) %all-to-all-start) | async-done | bytes 12582944 | tf_op jit(solution)/shard_map/all_to_all | solution.py:48
  220.5 8.5 fusion.21
  229.0 8.5 fusion.20
  237.6 13.7 bitcast_convert_fusion
  251.3 13.7 bitcast_convert_fusion.1
  264.9 44.7 %pad_maximum_fusion = bf16[2048,16384]{1,0:T(8,128)(2,1)} fusion(bf16[2048,8192]{1,0:T(8,128)(2,1)} %bitcast_convert_fusion, bf16[2048,8192]{1,0:T(8,128)(2,1)} %bitcast_convert_fusion.1), kind=kLoop, calls=%fused_computation.9 | loop fusion | flops 134217728 | bytes 134217728 | tf_op jit(solution)/shard_map/concatenate | solution.py:49
  309.7 11.1 all-to-all-start.2
  320.8 3.5 gather_fusion.4
  324.3 3.8 sort.35
  328.7 4.9 fusion.13
  333.6 3.5 gather_fusion.5
  337.2 34.1 %fusion.19 = f32[512,8192]{1,0:T(8,128)} fusion(bf16[512,3072]{1,0:T(8,128)(2,1)} %param.15, bf16[3072,8192]{1,0:T(8,128)(2,1)} %param.17), kind=kOutput, calls=%fused_computation.64 | convolution fusion | flops 25769803776 | bytes 70254592 | tf_op jit(solution)/shard_map/dot_general | solution.py:51
  371.3 672.1 %all-to-all-done.2 = bf16[8,256,16384]{2,1,0:T(8,128)(2,1)} async-done(((bf16[8,256,16384]{2,1,0:T(8,128)(2,1)}), bf16[8,256,16384]{2,1,0:T(8,128)(2,1)}, u32[]{:S(2)}, u32[]{:S(2)}) %all-to-all-start.2) | async-done | bytes 67108896 | tf_op jit(solution)/shard_map/all_to_all | solution.py:50
  1043.4 40.8 %gather_fusion.1 = bf16[512,16384]{1,0:T(8,128)(2,1)} fusion(bf16[2048,16384]{1,0:T(8,128)(2,1)} %bitcast.23, s32[1024]{0:T(1024)S(1)} %pad_clamp_fusion), kind=kCustom, calls=%fused_computation.5 | custom fusion | bytes 33556480 | tf_op jit(solution)/shard_map/jit(_take)/gather | solution.py:50
  1084.2 14.2 broadcast_select_fusion.1
  1098.4 40.5 %multiply_convert_fusion = bf16[512,8192]{1,0:T(8,128)(2,1)} fusion(f32[512,8192]{1,0:T(8,128)} %fusion.19, bf16[512,3072]{1,0:T(8,128)(2,1)} %param.15, bf16[3072,8192]{1,0:T(8,128)(2,1)} %param.18, bf16[512,16384]{1,0:T(8,128)(2,1)} %broadcast_select_fusion.1), kind=kOutput, calls=%fused_computation.14 | convolution fusion | flops 25811746816 | bytes 95420416 | tf_op jit(solution)/shard_map/dot_general | solution.py:52
  1138.9 58.4 %gather_fusion.2 = bf16[2048,8192]{1,0:T(8,128)(2,1)} fusion(bf16[512,8192]{1,0:T(8,128)(2,1)} %multiply_convert_fusion, s32[2048]{0:T(1024)S(1)} %copy-done.14), kind=kCustom, calls=%fused_computation.6 | custom fusion | bytes 67117056 | tf_op jit(solution)/shard_map/jit(_take)/gather | solution.py:54
  1197.3 22.8 %broadcast_select_fusion = bf16[8,256,8192]{2,1,0:T(8,128)(2,1)} fusion(bf16[8,256,8192]{2,1,0:T(8,128)(2,1)} %bitcast.58, pred[8,256]{1,0:T(8,128)(4,1)S(1)} %copy-done.18), kind=kLoop, calls=%fused_computation.12 | loop fusion | flops 16777216 | bytes 67110912 | tf_op jit(solution)/shard_map/jit(_take)/select_n | solution.py:54
  1220.1 375.6 %all_to_all.51 = bf16[8,256,8192]{2,1,0:T(8,128)(2,1)} all-to-all(bf16[8,256,8192]{2,1,0:T(8,128)(2,1)} %broadcast_select_fusion), channel_id=1, replica_groups=mesh['rep'=1,'dp'=16,'ad'=8] {'ad'}, dimensions={0} | all-to-all | bytes 67108864 | tf_op jit(solution)/shard_map/all_to_all | solution.py:54
  1595.7 16.2 fusion.22
  1611.9 3.7 bitcast_convert_fusion.2
  1615.6 143.1 %all_to_all.52 = bf16[8,256,3072]{2,1,0:T(8,128)(2,1)} all-to-all(bf16[8,256,3072]{2,1,0:T(8,128)(2,1)S(1)} %bitcast.60), channel_id=1, replica_groups=mesh['rep'=1,'dp'=16,'ad'=8] {'ad'}, dimensions={0} | all-to-all | bytes 25165824 | tf_op jit(solution)/shard_map/all_to_all | solution.py:55
  1758.8 13.2 gather_fusion.3
  1772.0 35.4 %add_convert_fusion = bf16[512,3072]{1,0:T(8,128)(2,1)} fusion(bf16[512,3072]{1,0:T(8,128)(2,1)} %param.15, bf16[512,8192]{1,0:T(8,128)(2,1)} %multiply_convert_fusion, bf16[8192,3072]{1,0:T(8,128)(2,1)} %param.19, bf16[512,3072]{1,0:T(8,128)(2,1)} %gather_fusion.3, pred[512]{0:T(512)(128)(4,1)S(1)} %copy-done.22), kind=kOutput, calls=%fused_computation.17 | convolution fusion | flops 25779240960 | bytes 68157952 | tf_op jit(solution)/shard_map/dot_general | solution.py:57
  (69 shorter events, 3.0 us)
Async XLA Ops:
  0.0 237.5 %copy-start = (bf16[2,32,8192]{2,1,0:T(8,128)(2,1)S(1)}, bf16[2,32,8192]{2,1,0:T(8,128)(2,1)}, u32[]{:S(2)}) copy-start(bf16[2,32,8192]{2,1,0:T(8,128)(2,1)} %param.23) | copy-start | bytes 3145732
  0.8 64.8 %copy-start.4 = (s32[512]{0:T(512)}, s32[512]{0:T(512)S(1)}, u32[]{:S(2)}) copy-start(s32[512]{0:T(512)S(1)} %get-tuple-element.16) | copy-start | bytes 6148
  5.1 0.5 copy-start.15
  9.5 56.1 %copy-start.2 = (s32[512]{0:T(512)}, s32[512]{0:T(512)S(1)}, u32[]{:S(2)}) copy-start(s32[512]{0:T(512)S(1)} %get-tuple-element.9) | copy-start | bytes 6148
  22.7 42.9 %copy-start.13 = (s32[2048]{0:T(1024)}, s32[2048]{0:T(1024)S(1)}, u32[]{:S(2)}) copy-start(s32[2048]{0:T(1024)S(1)} %broadcast_clamp_fusion) | copy-start | bytes 24580
  34.5 42.1 %all-to-all-start.1 = ((s32[8,256,1]{1,2,0:T(1,128)}), s32[8,256,1]{1,2,0:T(1,128)S(1)}, u32[]{:S(2)}, u32[]{:S(2)}) async-start(s32[8,256,1]{1,2,0:T(1,128)} %bitcast.15), calls=%async_computation.1 | async-start | bytes 16384 | tf_op jit(solution)/shard_map/all_to_all | solution.py:39
  40.3 25.3 %copy-start.17 = (pred[8,256]{1,0:T(8,128)(4,1)}, pred[8,256]{1,0:T(8,128)(4,1)S(1)}, u32[]{:S(2)}) copy-start(pred[8,256]{1,0:T(8,128)(4,1)S(1)} %broadcast_in_dim.85) | copy-start | bytes 6148
  76.5 144.0 %copy-start.9 = (bf16[2,3072,32]{1,2,0:T(8,128)(2,1)S(1)}, bf16[2,3072,32]{1,2,0:T(8,128)(2,1)}, u32[]{:S(2)}) copy-start(bf16[2,3072,32]{1,2,0:T(8,128)(2,1)} %param.22) | copy-start | bytes 1179652
  76.5 152.5 %copy-start.10 = (bf16[2,3072,32]{1,2,0:T(8,128)(2,1)S(1)}, bf16[2,3072,32]{1,2,0:T(8,128)(2,1)}, u32[]{:S(2)}) copy-start(bf16[2,3072,32]{1,2,0:T(8,128)(2,1)} %param.20) | copy-start | bytes 1179652
  76.5 144.0 %all-to-all-start = ((bf16[8,256,3072]{2,1,0:T(8,128)(2,1)}), bf16[8,256,3072]{2,1,0:T(8,128)(2,1)}, u32[]{:S(2)}, u32[]{:S(2)}) async-start(bf16[8,256,3072]{2,1,0:T(8,128)(2,1)} %broadcast_select_fusion.2), calls=%async_computation | async-start | bytes 25165824 | tf_op jit(solution)/shard_map/all_to_all | solution.py:48
  82.2 169.1 %copy-start.11 = (bf16[2048,2]{0,1:T(2,128)(2,1)}, bf16[2048,2]{0,1:T(2,128)(2,1)S(1)}, u32[]{:S(2)}) copy-start(bf16[2048,2]{0,1:T(2,128)(2,1)S(1)} %compare_convert_fusion) | copy-start | bytes 24580
  237.5 13.7 copy-start.6
  309.6 11.1 copy-start.3
  309.6 11.1 copy-start.5
  309.6 18.4 %copy-start.16 = (s32[8]{0:T(128)S(1)}, s32[8]{0:T(128)}, u32[]{:S(2)}) copy-start(s32[8]{0:T(128)} %copy-done.15) | copy-start | bytes 100
  309.7 733.7 %all-to-all-start.2 = ((bf16[8,256,16384]{2,1,0:T(8,128)(2,1)}), bf16[8,256,16384]{2,1,0:T(8,128)(2,1)}, u32[]{:S(2)}, u32[]{:S(2)}) async-start(bf16[8,256,16384]{2,1,0:T(8,128)(2,1)} %bitcast.22), calls=%async_computation.2 | async-start | bytes 134217728 | tf_op jit(solution)/shard_map/all_to_all | solution.py:50
  337.2 747.1 %copy-start.21 = (pred[512]{0:T(512)(128)(4,1)}, pred[512]{0:T(512)(128)(4,1)S(1)}, u32[]{:S(2)}) copy-start(pred[512]{0:T(512)(128)(4,1)S(1)} %get-tuple-element.11) | copy-start | bytes 1540
  337.2 706.2 %copy-start.19 = (s32[1024]{0:T(1024)}, s32[1024]{0:T(1024)S(1)}, u32[]{:S(2)}) copy-start(s32[1024]{0:T(1024)S(1)} %pad_clamp_fusion) | copy-start | bytes 12292
  1098.4 40.5 %copy-start.14 = (s32[2048]{0:T(1024)S(1)}, s32[2048]{0:T(1024)}, u32[]{:S(2)}) copy-start(s32[2048]{0:T(1024)} %copy-done.13) | copy-start | bytes 24580
  1138.9 58.4 %copy-start.18 = (pred[8,256]{1,0:T(8,128)(4,1)S(1)}, pred[8,256]{1,0:T(8,128)(4,1)}, u32[]{:S(2)}) copy-start(pred[8,256]{1,0:T(8,128)(4,1)} %copy-done.17) | copy-start | bytes 6148
  1220.1 375.6 %copy-start.7 = (bf16[2,8192,32]{1,2,0:T(8,128)(2,1)S(1)}, bf16[2,8192,32]{1,2,0:T(8,128)(2,1)}, u32[]{:S(2)}) copy-start(bf16[2,8192,32]{1,2,0:T(8,128)(2,1)} %param.24) | copy-start | bytes 3145732
  1595.7 16.2 copy-start.8
  1595.7 16.2 copy-start.12
  1615.6 143.1 %copy-start.20 = (s32[1024]{0:T(1024)S(1)}, s32[1024]{0:T(1024)}, u32[]{:S(2)}) copy-start(s32[1024]{0:T(1024)} %copy-done.19) | copy-start | bytes 12292
  1758.7 13.2 copy-start.22
  1772.0 35.4 %copy-start.1 = (bf16[2,32,8192]{2,1,0:T(8,128)(2,1)S(1)}, bf16[2,32,8192]{2,1,0:T(8,128)(2,1)}, u32[]{:S(2)}) copy-start(bf16[2,32,8192]{2,1,0:T(8,128)(2,1)} %param.23) | copy-start | bytes 3145732
where the time goes:
time: 1810 us
  waiting for transfers between devices  811 us (45%)
  blocking collectives  519 us (29%)
  matrix products  174 us (10%)
  local copies, waits for them, and re-layouts  170 us (9%)
  other arithmetic  111 us (6%)
  starting transfers between devices  22.5 us (1%)
    all_to_all x1, waiting for transfers between devices, local_step(): lax.all_to_all(gu_delta, 'ad', 0, 0, tiled=True)  672 us
    all_to_all x1, blocking collectives, local_step(): lax.all_to_all(jnp.take(hidden, send_rows, axis=0), 'ad', 0, 0, tiled=True)  376 us
    all_to_all x1, blocking collectives, local_step(): lax.all_to_all(low_rank(h_recv, a_down, b_down), 'ad', 0, 0, tiled=True)  143 us
    all_to_all x1, waiting for transfers between devices, local_step(): lax.all_to_all(jnp.take(x_rows, send_rows, axis=0), 'ad', 0, 0, tiled=True)  138 us
    gather x1, local copies, waits for them, and re-layouts, local_step(): jnp.take(hidden, send_rows, axis=0)  58.4 us
    concatenate x1, other arithmetic, local_step(): jnp.concatenate([low_rank(x_recv, a_gate, b_gate), low_rank(x_recv, a_up,...  44.7 us
    gather x1, local copies, waits for them, and re-layouts, local_step(): jnp.take(lax.all_to_all(gu_delta, 'ad', 0, 0, tiled=True), token_slot, ax...  40.8 us
    dot_general x1, matrix products, local_step(): jnp.dot(x_rows, w_up, preferred_element_type=jnp.float32)  40.5 us
  transfers between devices with their start and end apart: 3, of which 2 were waited for; matrix products, arithmetic and copies ran while one was open for 5% of the time, Pallas kernels for 0%

commit v1 on v0

v1 whole, which is shorter than its diff:
```python
import functools

import jax
import jax.numpy as jnp
from jax import lax
from jax.experimental import pallas as pl
from jax.experimental.pallas import tpu as pltpu
from jax.sharding import PartitionSpec as P

LORA_ALPHA = 32
MESH = pl.DeviceIdType.MESH
CHUNK = 1024
TILE = 256
SLOTS = 4
PEND = 10
AHEAD = 3
LAGS = (1, 3, 5, 6)
RING = 4


def kernel(scale, rank, x_hbm, ids_ref, wg_hbm, wu_hbm, wd_hbm, ag_hbm, au_hbm, bg_hbm, bu_hbm, ad_hbm, bd_hbm,
           out_hbm, x_v, gath, hid, low, load_sem, r1, r2, r3, r5, r7, send_sem, wsem, xsem, osem):
    rows, d_model = x_v.shape
    d_ff = hid.shape[1]
    n_chunks, n_rank, _ = gath.shape
    own_rows = ag_hbm.shape[0]
    half, quarter = own_rows // 2, own_rows // 4
    n_a = 2 * d_model // CHUNK
    n_b = 2 * d_ff // CHUNK
    n_d = d_ff // CHUNK
    n_tiles = d_ff // TILE
    n_out = d_model // TILE
    hc = CHUNK // 2

    dp = lax.axis_index("dp")
    ad = lax.axis_index("ad")
    x, core = ad // 2, ad % 2
    z, y = dp // RING, dp % RING
    par = y % 2
    xp = {"dp": dp, "ad": ((x + 1) % RING) * 2 + core}
    xm = {"dp": dp, "ad": ((x + RING - 1) % RING) * 2 + core}
    yp = {"dp": z * RING + (y + 1) % RING, "ad": ad}
    ym = {"dp": z * RING + (y + RING - 1) % RING, "ad": ad}
    sib = {"dp": dp, "ad": x * 2 + (1 - core)}

    def row_of(owner_x):
        return (owner_x * 2 + core) * own_rows

    r_own = row_of(x)
    r_m = row_of((x + RING - 1) % RING)
    r_p = row_of((x + 1) % RING)
    r_o = row_of((x + 2) % RING)
    mine = par * half
    other = (1 - par) * half

    def looped(n, fn):
        lax.fori_loop(0, n, lambda i, c: (fn(i), c)[1], 0)

    def up_loads(ring, t, slot):
        cols = pl.ds(pl.multiple_of(t * TILE, TILE), TILE)
        pltpu.make_async_copy(wg_hbm.at[:, cols], ring.at[slot], wsem.at[slot]).start()
        pltpu.make_async_copy(wu_hbm.at[:, cols], ring.at[slot + 1], wsem.at[slot + 1]).start()

    def up_wait(ring, slot):
        pltpu.make_async_copy(wg_hbm.at[:, pl.ds(0, TILE)], ring.at[slot], wsem.at[slot]).wait()

    def wide(low_rows, b_all):
        return (scale * jnp.dot(low_rows, b_all, preferred_element_type=jnp.float32)).astype(jnp.bfloat16).astype(
            jnp.float32)

    def select(proj):
        col = lax.broadcasted_iota(jnp.int32, proj.shape, 1) // rank
        keep = ids_ref[...] == col
        return jnp.where(keep, proj, 0.0).astype(jnp.bfloat16)

    def dot_nt(lhs, rhs):
        return lax.dot_general(lhs, rhs, (((1,), (1,)), ((), ())), preferred_element_type=jnp.float32)

    def phase1(ring, pend):
        barrier = pltpu.get_barrier_semaphore()
        for dev in (xp, xm, yp, ym, sib):
            pl.semaphore_signal(barrier, inc=1, device_id=dev, device_id_type=MESH)

        x_copy = pltpu.make_async_copy(x_hbm, x_v, xsem.at[0])
        x_copy.start()

        def span(c, row, n):
            return gath.at[c, pl.ds(pl.multiple_of(row, quarter), n), :]

        up_loads(ring, 0, 0)
        own = pl.ds(pl.multiple_of(r_own, own_rows), own_rows)

        def load_pair(c, k, first, second):
            cols = pl.ds(pl.multiple_of(k * hc, hc), hc)
            pltpu.make_async_copy(first.at[:, cols], gath.at[c, own, pl.ds(0, hc)], load_sem.at[c]).start()
            pltpu.make_async_copy(second.at[:, cols], gath.at[c, own, pl.ds(hc, hc)], load_sem.at[c]).start()

        def load_one(c, k, src):
            cols = pl.ds(pl.multiple_of(k * CHUNK, CHUNK), CHUNK)
            pltpu.make_async_copy(src.at[:, cols], gath.at[c, own, :], load_sem.at[c]).start()

        looped(n_a, lambda k: load_pair(k, k, ag_hbm, au_hbm))
        up_loads(ring, 1, 2)
        looped(n_b, lambda k: load_pair(n_a + k, k, bg_hbm, bu_hbm))
        looped(n_d, lambda k: load_one(n_a + n_b + k, k, ad_hbm))
        looped(n_chunks - n_a - n_b - n_d, lambda k: load_one(n_a + n_b + n_d + k, k, bd_hbm))

        def rcopy(c, row, n, sem, dev):
            return pltpu.make_async_remote_copy(src_ref=span(c, row, n), dst_ref=span(c, row, n), send_sem=send_sem.at[c],
                                                recv_sem=sem.at[c], device_id=dev, device_id_type=MESH)

        def send(c, row, n, sem, dev):
            rcopy(c, row, n, sem, dev).start()

        def arrived(c, n, sem):
            rcopy(c, 0, n, sem, sib).wait_recv()

        def stage0(c):
            pltpu.make_async_copy(bd_hbm.at[:, pl.ds(0, CHUNK)], gath.at[c, own, :], load_sem.at[c]).wait()
            send(c, r_own + mine, half, r1, xp)
            send(c, r_own + mine, half, r2, xm)
            send(c, r_own, own_rows, r7, sib)

        def stage1(c):
            arrived(c, half, r1)
            arrived(c, half, r2)
            send(c, r_m + mine, quarter, r3, xp)
            send(c, r_p + mine + quarter, quarter, r3, xm)
            for r in (r_m, r_p):
                send(c, r + mine, quarter, r5, yp)
                send(c, r + mine + quarter, quarter, r5, ym)
                send(c, r + mine, half, r7, sib)

        def stage2(c):
            arrived(c, half, r3)
            send(c, r_o + mine, quarter, r5, yp)
            send(c, r_o + mine + quarter, quarter, r5, ym)
            send(c, r_o + mine, half, r7, sib)

        def stage3(c):
            arrived(c, 3 * half, r5)
            for r in (r_m, r_p, r_o):
                send(c, r + other, half, r7, sib)

        def stage4(c):
            arrived(c, RING * own_rows, r7)

        def step(n):
            for c, fn in ((n + AHEAD, stage0), (n - LAGS[0], stage1), (n - LAGS[1], stage2), (n - LAGS[2], stage3),
                          (n - LAGS[3], stage4)):
                pl.when(jnp.logical_and(c >= 0, c < n_chunks))(functools.partial(fn, c))

        pl.semaphore_wait(barrier, 5)
        for c in range(AHEAD):
            stage0(c)
        x_copy.wait()

        def base(t):
            slot = 2 * (t % 2)
            at = t % PEND
            pend[at, 0] = jnp.dot(x_v[...], ring[slot], preferred_element_type=jnp.float32)
            pend[at, 1] = jnp.dot(x_v[...], ring[slot + 1], preferred_element_type=jnp.float32)

        def take(t):
            slot = 2 * (t % 2)
            up_wait(ring, slot)
            up_wait(ring, slot + 1)

        def refill(t):
            @pl.when(t + 2 < n_tiles)
            def _():
                up_loads(ring, t + 2, 2 * (t % 2))

        per = hc // TILE

        def finish(t):
            c = n_a + t // per
            off = pl.multiple_of((t % per) * TILE, TILE)
            at = t % PEND
            gate = pend[at, 0] + wide(low[0], gath[c, :, pl.ds(off, TILE)])
            up = pend[at, 1] + wide(low[1], gath[c, :, pl.ds(pl.multiple_of(hc + off, TILE), TILE)])
            hid[:, pl.ds(pl.multiple_of(t * TILE, TILE), TILE)] = (jax.nn.silu(gate) * up).astype(jnp.bfloat16)

        def first_loop(n):
            step(n)
            take(n)
            base(n)
            refill(n)

        looped(PEND, first_loop)

        for i in range(PEND, n_a + LAGS[3]):
            pl.when(i >= PEND)(functools.partial(step, jnp.int32(i)))
        extra = max(PEND, n_a + LAGS[3]) - PEND

        for kind in range(2):
            acc = None
            for k in range(n_a):
                part = dot_nt(x_v[:, k * hc:(k + 1) * hc], gath[k, :, kind * hc:(kind + 1) * hc])
                acc = part if acc is None else acc + part
            low[kind] = select(acc)

        def second_loop(i):
            n = i + PEND
            step(n + extra)
            take(n)
            finish(n - PEND)
            base(n)
            refill(n)

        looped(n_tiles - PEND, second_loop)
        def third_loop(i):
            n = i + n_tiles
            step(n + extra)
            finish(n - PEND)

        looped(PEND, third_loop)
        for i in range(n_tiles + PEND + extra, n_chunks + LAGS[3]):
            step(jnp.int32(i))

    pl.run_scoped(phase1, pltpu.VMEM((SLOTS, d_model, TILE), jnp.bfloat16),
                  pltpu.VMEM((PEND, 2, rows, TILE), jnp.float32))

    def phase2(wd_v, acc):
        def down_copy(n):
            cols = pl.ds(pl.multiple_of(n * TILE, TILE), TILE)
            return pltpu.make_async_copy(wd_hbm.at[:, cols], wd_v.at[n % 2], wsem.at[n % 2])

        down_copy(0).start()
        down_copy(1).start()
        acc[...] = jnp.zeros_like(acc)

        def low_down(k):
            lhs = hid[:, pl.ds(pl.multiple_of(k * CHUNK, CHUNK), CHUNK)]
            acc[...] += dot_nt(lhs, gath[n_a + n_b + k])

        looped(n_d, low_down)
        low[0] = select(acc[...])
        per_e = CHUNK // TILE

        def out_copy(n):
            cols = pl.ds(pl.multiple_of(n * TILE, TILE), TILE)
            return pltpu.make_async_copy(x_v.at[:, cols], out_hbm.at[:, cols], osem.at[n])

        def down(n):
            down_copy(n).wait()
            cols = pl.ds(pl.multiple_of(n * TILE, TILE), TILE)
            off = pl.multiple_of((n % per_e) * TILE, TILE)
            delta = wide(low[0], gath[n_a + n_b + n_d + n // per_e, :, pl.ds(off, TILE)])
            total = jnp.dot(hid[...], wd_v[n % 2], preferred_element_type=jnp.float32) + delta
            x_v[:, cols] = (x_v[:, cols].astype(jnp.float32) + total).astype(jnp.bfloat16)
            out_copy(n).start()

            @pl.when(n + 2 < n_out)
            def _():
                down_copy(n + 2).start()

        looped(n_out, down)
        looped(n_out, lambda n: out_copy(n).wait())
        sent = 7 * own_rows
        looped(n_chunks, lambda c: pltpu.make_async_remote_copy(
            src_ref=gath.at[c, pl.ds(0, sent), :], dst_ref=gath.at[c, pl.ds(0, sent), :], send_sem=send_sem.at[c],
            recv_sem=r7.at[c], device_id=sib, device_id_type=MESH).wait_send())

    pl.run_scoped(phase2, pltpu.VMEM((2, d_ff, TILE), jnp.bfloat16), pltpu.VMEM((rows, n_rank), jnp.float32))


def solution(mesh):
    group = mesh.shape["ad"]
    tok_axes = ("rep", "dp", "ad")
    row_spec = P(tok_axes, None)
    owned = P("ad", None, None)

    def local_step(x_rows, adapter_id, w_gate, w_up, w_down, a_gate, b_gate, a_up, b_up, a_down, b_down):
        n_rows, d_model = x_rows.shape
        d_ff = w_gate.shape[1]
        n_local, _, rank = a_gate.shape
        local = n_local * rank
        n_rank = group * local
        n_chunks = (3 * d_model + 3 * d_ff) // CHUNK

        def cols_of(mat):
            return mat.transpose(0, 2, 1).reshape(local, mat.shape[1])

        def rows_of(mat):
            return mat.reshape(local, mat.shape[2])

        dma = lambda n: pltpu.SemaphoreType.DMA((n,))
        anyspec = pl.BlockSpec(memory_space=pl.ANY)
        flops = 2 * n_rows * (3 * d_model * d_ff + n_rank * (3 * d_model + 3 * d_ff))
        call = pl.pallas_call(
            functools.partial(kernel, LORA_ALPHA / rank, rank),
            out_shape=jax.ShapeDtypeStruct((n_rows, d_model), x_rows.dtype),
            in_specs=[anyspec, pl.BlockSpec(memory_space=pltpu.VMEM)] + [anyspec] * 9,
            out_specs=anyspec,
            scratch_shapes=[
                pltpu.VMEM((n_rows, d_model), jnp.bfloat16),
                pltpu.VMEM((n_chunks, n_rank, CHUNK), jnp.bfloat16),
                pltpu.VMEM((n_rows, d_ff), jnp.bfloat16),
                pltpu.VMEM((2, n_rows, n_rank), jnp.bfloat16),
                dma(n_chunks), dma(n_chunks), dma(n_chunks), dma(n_chunks), dma(n_chunks), dma(n_chunks),
                dma(n_chunks), dma(SLOTS), dma(1), dma(d_model // TILE),
            ],
            compiler_params=pltpu.CompilerParams(collective_id=0, has_side_effects=True, vmem_limit_bytes=67043328),
            cost_estimate=pl.CostEstimate(flops=flops, bytes_accessed=6 * d_model * d_ff, transcendentals=n_rows * d_ff),
            name="lora_mlp",
        )
        return call(x_rows, adapter_id.reshape(n_rows, 1), w_gate, w_up, w_down, cols_of(a_gate), cols_of(a_up),
                    rows_of(b_gate), rows_of(b_up), cols_of(a_down), rows_of(b_down))

    return jax.shard_map(local_step, mesh=mesh,
                         in_specs=(row_spec, P(tok_axes), P(), P(), P(), owned, owned, owned, owned, owned, owned),
                         out_specs=row_spec, check_vma=False)
```

time: 1810 us -> 142 us (0.08)
  waiting for transfers between devices: 811 us -> 0 us
  blocking collectives: 519 us -> 0 us
  matrix products: 174 us -> 0 us
  local copies, waits for them, and re-layouts: 170 us -> 5.29 us
  Pallas kernels: 0 us -> 136 us
  other arithmetic: 111 us -> 0 us
  starting transfers between devices: 22.5 us -> 0 us
    all_to_all x3 -> x0, waiting for transfers between devices: 811 us -> none  [the longest x1 672 us: local_step(): lax.all_to_all(gu_delta, 'ad', 0, 0, tiled=True)]
    all_to_all x2 -> x0, blocking collectives: 519 us -> none  [the longest x1 376 us: local_step(): lax.all_to_all(jnp.take(hidden, send_rows, axis=0), 'ad', 0, 0, tiled=True)]
    gather x9 -> x0, local copies, waits for them, and re-layouts: 170 us -> none  [the longest x1 58.4 us: local_step(): jnp.take(hidden, send_rows, axis=0)]
    dot_general x6 -> x0, matrix products: 141 us -> none  [the longest x1 40.5 us: local_step(): jnp.dot(x_rows, w_up, preferred_element_type=jnp.float32)]
    pallas_call x0 -> x1, Pallas kernels: none -> 136 us  [local_step(): call(x_rows, adapter_id.reshape(n_rows, 1), w_gate, w_up, w_down, cols_of...]
    select_n x6 -> x0, other arithmetic: 48.5 us -> none  [the longest x1 22.8 us: local_step(): jnp.take(hidden, send_rows, axis=0)]
    concatenate x1 -> x0, other arithmetic: 44.7 us -> none  [local_step(): jnp.concatenate([low_rank(x_recv, a_gate, b_gate), low_rank(x_recv, a_up,...]
    unnamed x3 -> x0, matrix products: 33.2 us -> none
  transfers between devices with their start and end apart: 3 -> 0, of which waited for: 2 -> 0; matrix products, arithmetic and copies ran while one was open for 5% -> 0% of each run, Pallas kernels for 0% -> 0%
where the time goes in v1:
time: 142 us
  Pallas kernels  136 us (96%)
  local copies, waits for them, and re-layouts  5.29 us (4%)
    pallas_call x1, Pallas kernels, local_step(): call(x_rows, adapter_id.reshape(n_rows, 1), w_gate, w_up, w_down, cols_of...  136 us
    unnamed x1, local copies, waits for them, and re-layouts  3.76 us

profile of v1, /device:TPU:1, one launch (start us, length us, event | category | flops | bytes accessed | tf_op | source)
XLA Modules:
  0.0 141.5 jit_solution(6906092130969047078)
XLA Ops:
  0.0 1.5 %copy.12.ids_ref = s32[512,1]{1,0:T(8,128)} copy(s32[512,1]{0,1:T(1,128)} %bitcast.13) | data formatting | bytes 4096 | tf_op jit(solution)/shard_map/reshape | solution.py:308
  1.5 136.2 %lora_mlp.1 = bf16[512,3072]{1,0:T(8,128)(2,1)} custom-call(bf16[512,3072]{1,0:T(8,128)(2,1)} %x_hbm.1, s32[512,1]{1,0:T(8,128)} %copy.12.ids_ref, bf16[3072,8192]{1,0:T(8,128)(2,1)} %wg_hbm.1, bf16[3072,8192]{1,0:T(8,128)(2,1)} %wu_hbm.1, bf16[8192,3072]{1,0:T(8,128)(2,1)} %wd_hbm.1, bf16[64,3072]{1,0:T(8,128)(2,1)} %bitcast.17, bf16[64,3072]{1,0:T(8,128)(2,1)} %bitcast.18, ...), custom_call_target="tpu_custom_call" | custom-call | flops 95026151424 | bytes 150994944 | tf_op jit(solution)/shard_map/lora_mlp/pallas_call | solution.py:308
  137.8 3.8 %copy.14 = bf16[512,3072]{1,0:T(8,128)(2,1)} copy(bf16[512,3072]{1,0:T(8,128)(2,1)} %lora_mlp.1) | data formatting | bytes 6291456
